TPU v7x, 32 devices: a whole 2x2x4 slice. The times are simulated.
32 devices in a mesh: rows: 8 (over y, x, core), grp: 4 (over z).
Axes of the slice: x: 2, y: 2, z: 4, core: 2. Of those that a mesh axis runs over, the one named last changes fastest.
Arguments:
- matrix: bfloat16 [24576, 16384], P(('rows', 'grp')), may hold values from -3000 to 3000, as said below
- keep_mask: int32 [16, 24576], P(None, ('rows', 'grp')), may hold values 0 or 1
Outputs:
- cosine: float32 [16384, 256], P(('rows', 'grp'))
Inputs may be any that keep to these rules, and one draw needn't show every extreme that they name: `matrix`: entries are real-valued; row and column magnitudes vary.
All inputs are finite; a program needn't handle non-finite values. No bound on the sum of `keep_mask` on one device may be relied on, other than what follows from the above.
Results may differ from a plain program's by a relative error of at most 0.0003.
Values sent between devices are 32-bit elements; how exact they have to be, the bound alone decides.
A program may use at most 192 MiB of HBM per device.

v0:
```python
import functools

import jax
import jax.numpy as jnp
from jax import lax
from jax.experimental import pallas as pl
from jax.experimental.pallas import tpu as pltpu
from jax.sharding import PartitionSpec as P

WINDOW = 256
STAT = 8
HEIGHT = WINDOW + STAT
SUB = 256
SLOTS = 4
MESH = pl.DeviceIdType.MESH
PIECES_XYZ = (32, 32, 24, 16, 16)
PIECES_YXZ = (32, 24, 24, 16, 16)
PIECES_Z = (("zxy", 16), ("zyx", 16))
EARLY = 2


class Piece:
    def __init__(self, start, height, order):
        self.start, self.height, self.order = start, height, order


def pieces():
    out, at = [], 0
    for order, height in (
        [("xyz", h) for h in PIECES_XYZ]
        + [("yxz", h) for h in PIECES_YXZ]
        + list(PIECES_Z)
    ):
        out.append((at, height, order))
        at += height
    assert at == HEIGHT
    made = [Piece(*p) for p in out]
    a = len(PIECES_XYZ)
    b = a + len(PIECES_YXZ)
    return made[:a], made[a:b], made[b:]


def phase_copies(order, phase, sizes):
    axis, fixed = order[phase], order[:phase]
    groups = [
        (dx, dy)
        for dx in reversed(range(sizes["x"]))
        for dy in reversed(range(sizes["y"]))
        if not ("x" in fixed and dx) and not ("y" in fixed and dy)
    ]
    kept = [g for g in groups if axis == "z" or g["xy".index(axis)] == 0]
    sent = []
    for d in range(1, sizes[axis]):
        if axis == "z":
            sent.append(kept)
        elif axis == "x":
            sent.append([(d, dy) for _, dy in kept])
        else:
            sent.append([(dx, d) for dx, _ in kept])
    return axis, kept, sent


def kernel(cfg, matrix_ref, keep_ref, out_ref, acc, sib_out, sib_in, mbuf, panel,
           masked, wst, load_sem, sib_send, sib_recv, send_sem, recv_sem, *bufs):
    X, Y, Z, tile, width, step = (
        cfg["x"], cfg["y"], cfg["z"], cfg["tile"], cfg["width"], cfg["step"]
    )
    span = Z * tile
    halves = span // step
    rows = lax.axis_index("rows")
    z = lax.axis_index("grp")
    c = lax.rem(rows, 2)
    x = lax.rem(rows // 2, X)
    y = rows // (2 * X)

    def device(yy, xx, cc, zz):
        return ((yy * X + xx) * 2 + cc, zz)

    def quad(g):
        return lax.rem(y + g[1], Y) * X + lax.rem(x + g[0], X)

    def peer(axis, d):
        if axis == "x":
            return device(y, lax.rem(x + d, X), c, z)
        if axis == "y":
            return device(lax.rem(y + d, Y), x, c, z)
        return device(y, x, c, lax.rem(z + d, Z))

    groups = [(dx, dy) for dx in reversed(range(X)) for dy in reversed(range(Y))]
    units = [(groups[0], h) for h in range(halves)]
    units += [(g, h) for h in range(halves) for g in groups[1:-1]]
    units += [(groups[-1], h) for h in range(halves)]
    steps = [(g, own, h) for g, h in units for own in (0, 1)]

    def base(s):
        g, own, h = s
        cc = c if own else 1 - c
        return pl.multiple_of((quad(g) * 2 + cc) * span + h * step, step)

    def load(i):
        return pltpu.make_async_copy(
            matrix_ref.at[:, pl.ds(base(steps[i]), step)],
            mbuf.at[i % SLOTS],
            load_sem.at[i % SLOTS],
        )

    window = pltpu.make_async_copy(
        matrix_ref.at[:, pl.ds(0, WINDOW)],
        mbuf.at[SLOTS - 1, :, pl.ds(0, WINDOW)],
        load_sem.at[SLOTS - 1],
    )
    window.start()
    for i in range(SLOTS - 1):
        load(i).start()

    peers = [device(y, x, 1 - c, z)]
    for axis, n in (("x", X), ("y", Y), ("z", Z)):
        peers += [peer(axis, d) for d in range(1, n)]
    barrier = pltpu.get_barrier_semaphore()
    for p in peers:
        pl.semaphore_signal(barrier, inc=1, device_id=p, device_id_type=MESH)

    window.wait()
    first = mbuf[SLOTS - 1, :, pl.ds(0, WINDOW)].astype(jnp.float32)
    window_sq = jnp.sum(first * first, axis=0, keepdims=True)
    panel[...] = first.T * keep_ref[pl.ds(0, 1), :].astype(jnp.float32)
    extra = (WINDOW + tile - 1) // tile
    wst[...] = jnp.zeros_like(wst)
    for e in range(extra):
        part = window_sq[:, e * tile : min(WINDOW, (e + 1) * tile)]
        for t in range(step // tile):
            wst[1 + e : 2 + e, t * tile : t * tile + part.shape[1]] = part
    load(SLOTS - 1).start()
    pl.semaphore_wait(barrier, len(peers))

    def compute(i, dst):
        load(i).wait()
        block = base(steps[i]) // width
        gate = keep_ref[pl.ds(block, 1), :].astype(jnp.float32)
        masked[...] = (panel[...] * gate).astype(jnp.bfloat16)
        first_row = lax.broadcasted_iota(jnp.int32, (STAT, SUB), 0) == 0

        def body(j, carry):
            at = pl.multiple_of(j * SUB, SUB)
            piece = mbuf[i % SLOTS, :, pl.ds(at, SUB)]
            dst[pl.ds(0, WINDOW), pl.ds(at, SUB)] = jnp.dot(
                masked[...], piece, preferred_element_type=jnp.float32
            )
            wide = piece.astype(jnp.float32)
            sq = jnp.sum(wide * wide, axis=0, keepdims=True)
            dst[pl.ds(WINDOW, STAT), pl.ds(at, SUB)] = jnp.where(
                first_row, sq, wst[:, pl.ds(at, SUB)]
            )
            return carry

        lax.fori_loop(0, step // SUB, body, 0, unroll=True)
        if i + SLOTS < len(steps):
            load(i + SLOTS).start()

    list_a, list_b, list_z = pieces()
    sends = {}
    buf_of = {}
    nsem = 0
    nbuf = 0
    for p in list_a + list_b + list_z:
        for phase in range(3):
            axis, kept, sent = phase_copies(p.order, phase, cfg)
            if not sent:
                buf_of[p, phase] = None
                sends[p, phase] = {}
                continue
            ref = bufs[nbuf]
            nbuf += 1
            buf_of[p, phase] = ref
            done = "z" in p.order[:phase]
            out = {}
            for d in range(1, cfg[axis] if axis != "z" else Z):
                for k, g in enumerate(sent[d - 1]):
                    if axis == "z":
                        to = lax.rem(z + d, Z)
                        cols = [pl.ds(pl.multiple_of(to * tile, tile), tile)]
                    elif done:
                        cols = [pl.ds(pl.multiple_of(z * tile, tile), tile)]
                    elif phase == 0:
                        cols = [pl.ds(h * step, step) for h in range(halves)]
                    else:
                        cols = [pl.ds(0, span)]
                    for h, part in enumerate(cols):
                        copy = functools.partial(
                            pltpu.make_async_remote_copy,
                            src_ref=acc.at[quad(g), pl.ds(p.start, p.height), part],
                            dst_ref=ref.at[d - 1, k, :, part]
                            if len(cols) > 1
                            else ref.at[d - 1, k],
                            send_sem=send_sem.at[nsem],
                            recv_sem=recv_sem.at[nsem],
                            device_id=peer(axis, d),
                            device_id_type=MESH,
                        )
                        nsem += 1
                        last = halves - 1 if len(cols) == 1 else h
                        out.setdefault((g, last), []).append(copy)
            sends[p, phase] = out

    def start(p, phase, g=None):
        for key, copies in sends[p, phase].items():
            if g is None or key == g:
                for copy in copies:
                    copy().start()

    def finish(p, phase):
        axis, kept, sent = phase_copies(p.order, phase, cfg)
        for copies in sends[p, phase].values():
            for copy in copies:
                copy().wait_recv()
        if not sent:
            return
        ref = buf_of[p, phase]
        if "z" in p.order[: phase + 1]:
            cols = pl.ds(pl.multiple_of(z * tile, tile), tile)
        else:
            cols = pl.ds(0, span)
        for k, g in enumerate(kept):
            where = (quad(g), pl.ds(p.start, p.height), cols)
            total = acc[where]
            for d in range(len(sent)):
                total = total + ref[d, k]
            acc[where] = total

    def sibling(n):
        return pltpu.make_async_remote_copy(
            src_ref=sib_out.at[n],
            dst_ref=sib_in.at[n],
            send_sem=sib_send.at[n],
            recv_sem=sib_recv.at[n],
            device_id=device(y, x, 1 - c, z),
            device_id_type=MESH,
        )

    early = list_z + [p for pair in zip(list_a[:EARLY], list_b[:EARLY]) for p in pair]

    def merge(n):
        g, h = units[n]
        q = quad(g)
        sibling(n).wait_recv()

        def add(j, carry):
            at = pl.multiple_of(j * 8, 8)
            acc[q, pl.ds(at, 8), pl.ds(h * step, step)] += sib_in[n, pl.ds(at, 8), :]
            return carry

        lax.fori_loop(0, HEIGHT // 8, add, 0)
        for p in early:
            start(p, 0, (g, h))

    for n, (g, h) in enumerate(units):
        compute(2 * n, sib_out.at[n])
        sibling(n).start()
        if n:
            merge(n - 1)
        compute(2 * n + 1, acc.at[quad(g), :, pl.ds(h * step, step)])
    merge(len(units) - 1)

    count = len(list_a)
    for t in range(count + 2):
        if EARLY <= t + 1 < count:
            start(list_a[t + 1], 0)
            start(list_b[t + 1], 0)
        if t < count:
            for p in (list_a[t], list_b[t]):
                finish(p, 0)
                start(p, 1)
        if t == 2 or t == 3:
            for p in list_z:
                finish(p, t - 2)
                start(p, t - 1)
        if 1 <= t <= count:
            for p in (list_a[t - 1], list_b[t - 1]):
                finish(p, 1)
                start(p, 2)
        if t == 4:
            for p in list_z:
                finish(p, 2)
        if t >= 2:
            for p in (list_a[t - 2], list_b[t - 2]):
                finish(p, 2)

    mine = acc[y * X + x, :, pl.ds(pl.multiple_of(z * tile, tile), tile)]
    own = 1.0 / jnp.sqrt(mine[WINDOW : WINDOW + 1, :] + 1e-06)
    parts = [
        mine[WINDOW + 1 + e : WINDOW + 2 + e, : min(tile, WINDOW - e * tile)]
        for e in range(extra)
    ]
    win = parts[0] if extra == 1 else jnp.concatenate(parts, axis=1)
    win = 1.0 / jnp.sqrt(win + 1e-06)
    out_ref[...] = (mine[:WINDOW, :] * own).T * win

    for n in range(len(units)):
        sibling(n).wait_send()
    for p in list_a + list_b + list_z:
        for phase in range(3):
            for copies in sends[p, phase].values():
                for copy in copies:
                    copy().wait_send()


def shards(matrix, keep_mask):
    depth, columns = matrix.shape
    blocks = keep_mask.shape[0]
    width = columns // blocks
    outer = lax.axis_size("rows")
    inner = lax.axis_size("grp")
    tile = columns // (outer * inner)
    cfg = {"x": 2, "y": outer // 4, "z": inner, "tile": tile, "width": width}
    span = inner * tile
    step = min(width, span)
    cfg["step"] = step
    quads = cfg["x"] * cfg["y"]
    links = quads * (span // step)
    bufs, nsem = [], 0
    for group in pieces():
        for p in group:
            for phase in range(3):
                axis, kept, sent = phase_copies(p.order, phase, cfg)
                if not sent:
                    continue
                cols = tile if "z" in p.order[: phase + 1] else span
                cuts = span // step if phase == 0 and p.order[0] != "z" else 1
                nsem += len(sent) * len(kept) * cuts
                bufs.append(
                    pltpu.VMEM((len(sent), len(kept), p.height, cols), jnp.float32)
                )
    return pl.pallas_call(
        functools.partial(kernel, cfg),
        out_shape=jax.ShapeDtypeStruct((tile, WINDOW), jnp.float32),
        in_specs=[
            pl.BlockSpec(memory_space=pl.ANY),
            pl.BlockSpec(memory_space=pltpu.VMEM),
        ],
        out_specs=pl.BlockSpec(memory_space=pltpu.VMEM),
        scratch_shapes=[
            pltpu.VMEM((quads, HEIGHT, span), jnp.float32),
            pltpu.VMEM((links, HEIGHT, step), jnp.float32),
            pltpu.VMEM((links, HEIGHT, step), jnp.float32),
            pltpu.VMEM((SLOTS, depth, step), jnp.bfloat16),
            pltpu.VMEM((WINDOW, depth), jnp.float32),
            pltpu.VMEM((WINDOW, depth), jnp.bfloat16),
            pltpu.VMEM((STAT, step), jnp.float32),
            pltpu.SemaphoreType.DMA((SLOTS,)),
            pltpu.SemaphoreType.DMA((links,)),
            pltpu.SemaphoreType.DMA((links,)),
            pltpu.SemaphoreType.DMA((nsem,)),
            pltpu.SemaphoreType.DMA((nsem,)),
        ]
        + bufs,
        compiler_params=pltpu.CompilerParams(
            collective_id=0, has_side_effects=True, vmem_limit_bytes=62 * 1024 * 1024
        ),
        cost_estimate=pl.CostEstimate(
            flops=2 * depth * columns * WINDOW,
            bytes_accessed=2 * depth * columns,
            transcendentals=0,
        ),
    )(matrix, keep_mask)


def solution(mesh):
    in_specs = (P(("rows", "grp"), None), P(None, ("rows", "grp")))
    out_specs = P(("rows", "grp"), None)
    return jax.shard_map(shards, mesh=mesh, in_specs=in_specs, out_specs=out_specs, check_vma=False)
```

profile of v0, /device:TPU:0, one launch (start us, length us, event | category | flops | bytes accessed | tf_op | source)
XLA Modules:
  0.0 90.5 jit_solution(1611755383591111012)
XLA Ops:
  0.0 88.6 %shard_map.28 = f32[512,256]{1,0:T(8,128)} custom-call(bf16[768,16384]{1,0:T(8,128)(2,1)} %matrix_ref.1, s32[16,768]{1,0:T(8,128)} %keep_ref.1), custom_call_target="tpu_custom_call" | custom-call | flops 6442450944 | bytes 25165824 | tf_op jit(solution)/shard_map/pallas_call | solution.py:333
  88.6 1.9 %copy.4 = f32[512,256]{1,0:T(8,128)} copy(f32[512,256]{1,0:T(8,128)} %shard_map.28) | data formatting | bytes 1048576
where the time goes:
time: 90.7 us; the launch traced here: 90.5 us
  Pallas kernels  88.6 us (98%)
  local copies, waits for them, and re-layouts  1.87 us (2%)
    pallas_call x1, Pallas kernels, shards(): pl.pallas_call(functools.partial(kernel, cfg), out_shape=jax.ShapeDtypeSt...  88.6 us
    unnamed x1, local copies, waits for them, and re-layouts  1.87 us

commit v1 on v0

v1 whole, which is shorter than its diff:
```python
import contextlib
import functools

import jax
import jax.numpy as jnp
from jax import lax
from jax.experimental import pallas as pl
from jax.experimental.pallas import tpu as pltpu
from jax.sharding import PartitionSpec as P

WINDOW = 256
LANES = 128
STAT = 8
SUB = 256
SLOTS = 4
STAGES = 4
RESTS = 8
MESH = pl.DeviceIdType.MESH
KINDS = {"A": "xyz", "B": "yxz", "C": "zxy", "D": "zyx", "E": "xzy", "F": "yzx"}
HEIGHTS = (
    ("A0", 24),
    ("B0", 24),
    ("C0", 16),
    ("D0", 8),
    ("E0", 16),
    ("F0", 16),
    ("A1", 16),
    ("A2", 16),
    ("A3", 16),
    ("B1", 24),
    ("B2", 16),
    ("B3", 16),
    ("C1", 8),
    ("E1", 24),
    ("F1", 16),
)
EARLY = ("A0", "B0", "C0", "D0", "E0", "F0")
STAT_KIND = "A"
LIMIT = 50
ORDER = (
    ("R", "R", 0),
    ("Z", "C0", 1),
    ("R", "R", 1),
    ("R", "R", 2),
    ("F", "A0", 0),
    ("F", "B0", 0),
    ("R", "R", 3),
    ("R", "R", 4),
    ("R", "R", 5),
    ("R", "R", 6),
    ("R", "R", 7),
    ("S", "E1", 0),
    ("S", "A1", 0),
    ("S", "T", 0),
    ("S", "F1", 0),
    ("Z", "C1", 0),
    ("S", "B1", 0),
    ("S", "A2", 0),
    ("S", "B2", 0),
    ("F", "E0", 0),
    ("Z", "E0", 0),
    ("Z", "E0", 1),
    ("Z", "E0", 2),
    ("F", "F0", 0),
    ("Z", "F0", 0),
    ("Z", "C1", 1),
    ("Z", "C1", 2),
    ("Z", "D0", 1),
    ("F", "B0", 1),
    ("Z", "B0", 0),
    ("Z", "B0", 1),
    ("F", "E1", 0),
    ("Z", "E1", 0),
    ("Z", "E1", 1),
    ("F", "B1", 0),
    ("S", "A3", 0),
    ("Z", "C0", 2),
    ("F", "A0", 1),
    ("Z", "A0", 0),
    ("Z", "F0", 1),
    ("S", "B3", 0),
    ("F", "F1", 0),
    ("Z", "F1", 0),
    ("Z", "B0", 2),
    ("Z", "A0", 1),
    ("F", "B2", 0),
    ("F", "A2", 0),
    ("Z", "D0", 2),
    ("F", "A1", 0),
    ("F", "T", 0),
    ("Z", "F1", 1),
    ("Z", "A0", 2),
    ("Z", "F0", 2),
    ("F", "B1", 1),
    ("Z", "B1", 0),
    ("Z", "B1", 1),
    ("F", "B3", 0),
    ("F", "A2", 1),
    ("Z", "A2", 0),
    ("F", "A3", 0),
    ("Z", "F1", 2),
    ("Z", "C0", 3),
    ("F", "A1", 1),
    ("F", "T", 1),
    ("Z", "A1", 0),
    ("Z", "T", 0),
    ("Z", "A1", 1),
    ("Z", "T", 1),
    ("F", "B2", 1),
    ("Z", "B2", 0),
    ("Z", "D0", 3),
    ("Z", "C1", 3),
    ("Z", "A2", 1),
    ("F", "A3", 1),
    ("Z", "A3", 0),
    ("F", "B3", 1),
    ("Z", "B3", 0),
    ("Z", "E1", 2),
    ("Z", "E1", 3),
    ("Z", "E0", 3),
    ("Z", "B1", 2),
    ("Z", "B1", 3),
    ("Z", "F0", 3),
    ("Z", "B2", 1),
    ("Z", "F1", 3),
    ("Z", "A0", 3),
    ("F", "C1", 1),
    ("Z", "A3", 1),
    ("F", "D0", 1),
    ("Z", "A2", 2),
    ("Z", "A2", 3),
    ("F", "C0", 1),
    ("Z", "B0", 3),
    ("F", "E1", 2),
    ("Z", "A1", 2),
    ("Z", "T", 2),
    ("Z", "B2", 2),
    ("Z", "B2", 3),
    ("F", "F0", 2),
    ("F", "F1", 2),
    ("Z", "B3", 1),
    ("F", "E0", 2),
    ("Z", "A1", 3),
    ("Z", "T", 3),
    ("Z", "A3", 2),
    ("Z", "A3", 3),
    ("Z", "B3", 2),
    ("F", "C0", 2),
    ("F", "C1", 2),
    ("F", "D0", 2),
    ("Z", "B3", 3),
)


def scope(name):
    return contextlib.nullcontext()


class Piece:
    def __init__(self, name, start, height, order, stat):
        self.name, self.start, self.height = name, start, height
        self.order, self.stat, self.kind = order, stat, name[0]


def pieces():
    out, at = {}, 0
    for name, height in HEIGHTS:
        out[name] = Piece(name, at, height, KINDS[name[0]], False)
        at += height
    assert at == WINDOW
    out["T"] = Piece("T", 0, STAT, KINDS[STAT_KIND], True)
    return out


def groups_of(sizes, order, phase):
    fixed = order[:phase]
    return [
        (dx, dy)
        for dx in reversed(range(sizes["x"]))
        for dy in reversed(range(sizes["y"]))
        if not ("x" in fixed and dx) and not ("y" in fixed and dy)
    ]


def exchange(sizes, order, phase):
    axis = order[phase]
    i = "xy".index(axis)
    kept = [g for g in groups_of(sizes, order, phase) if g[i] == 0]
    sent = [
        [(d, g[1]) if axis == "x" else (g[0], d) for g in kept]
        for d in range(1, sizes[axis])
    ]
    return kept, sent


def buffers(sizes, tile):
    out = []
    for p in pieces().values():
        unit = LANES if p.stat else tile
        for phase, axis in enumerate(p.order):
            if axis == "z":
                n = len(groups_of(sizes, p.order, phase))
                for way in ("up", "down"):
                    shape = (max(1, sizes["z"] - 1), n, p.height, unit)
                    out.append(((p.name, way), shape))
            else:
                kept, sent = exchange(sizes, p.order, phase)
                cols = unit if "z" in p.order[:phase] else sizes["z"] * unit
                shape = (max(1, len(sent)), len(kept), p.height, cols)
                out.append(((p.name, phase), shape))
    return out


def semaphores(sizes):
    recv, send = {}, {}
    for p in pieces().values():
        for phase, axis in enumerate(p.order):
            send.setdefault((p.kind, phase), len(send))
            if axis == "z":
                for t in range(sizes["z"] - 1):
                    recv[p.name, "up", t + 1] = len(recv)
                    recv[p.name, "down", t] = len(recv)
            else:
                recv[p.name, phase] = len(recv)
    return recv, send


def kernel(cfg, matrix_ref, keep_hbm, out_ref, acc, stat, sib_out, sib_in, stat_out,
           stat_in, mbuf, keep_ref, panel, masked, load_sem, keep_sem, sib_send,
           sib_recv, send_sem, recv_sem, *bufs):
    X, Y, Z, tile, width, step = (
        cfg["x"], cfg["y"], cfg["z"], cfg["tile"], cfg["width"], cfg["step"]
    )
    span = Z * tile
    halves = span // step
    per = step // tile
    rows = lax.axis_index("rows")
    z = lax.axis_index("grp")
    c = lax.rem(rows, 2)
    x = lax.rem(rows // 2, X)
    y = rows // (2 * X)

    def device(yy, xx, cc, zz):
        return ((yy * X + xx) * 2 + cc, zz)

    def quad(g):
        return lax.rem(y + g[1], Y) * X + lax.rem(x + g[0], X)

    def peer(axis, d):
        if axis == "x":
            return device(y, lax.rem(x + d, X), c, z)
        return device(lax.rem(y + d, Y), x, c, z)

    peers = [device(y, x, 1 - c, z)]
    for axis, n in (("x", X), ("y", Y)):
        peers += [peer(axis, d) for d in range(1, n)]
    barrier = pltpu.get_barrier_semaphore()
    for p in peers:
        pl.semaphore_signal(barrier, inc=1, device_id=p, device_id_type=MESH)

    @pl.when(z > 0)
    def _():
        pl.semaphore_signal(
            barrier, inc=1, device_id=device(y, x, c, z - 1), device_id_type=MESH
        )

    @pl.when(z < Z - 1)
    def _():
        pl.semaphore_signal(
            barrier, inc=1, device_id=device(y, x, c, z + 1), device_id_type=MESH
        )

    def await_peers():
        n = len(peers) + jnp.where(z > 0, 1, 0) + jnp.where(z < Z - 1, 1, 0)
        pl.semaphore_wait(barrier, n)

    groups = [(dx, dy) for dx in reversed(range(X)) for dy in reversed(range(Y))]
    units = [(groups[0], h) for h in range(halves)]
    units += [(g, h) for h in range(halves) for g in groups[1:-1]]
    units += [(groups[-1], h) for h in range(halves)]
    steps = [(g, own, h) for g, h in units for own in (0, 1)]

    def base(s):
        g, own, h = s
        cc = c if own else 1 - c
        return pl.multiple_of((quad(g) * 2 + cc) * span + h * step, step)

    def load(i):
        return pltpu.make_async_copy(
            matrix_ref.at[:, pl.ds(base(steps[i]), step)],
            mbuf.at[i % SLOTS],
            load_sem.at[i % SLOTS],
        )

    window = pltpu.make_async_copy(
        matrix_ref.at[:, pl.ds(0, WINDOW)],
        mbuf.at[SLOTS - 1, :, pl.ds(0, WINDOW)],
        load_sem.at[SLOTS - 1],
    )
    keep = pltpu.make_async_copy(keep_hbm, keep_ref, keep_sem)
    window.start()
    keep.start()
    for i in range(SLOTS - 1):
        load(i).start()

    with scope("head"):
        window.wait()
        keep.wait()
        first = mbuf[SLOTS - 1, :, pl.ds(0, WINDOW)].astype(jnp.float32)
        window_sq = jnp.sum(first * first, axis=0, keepdims=True)
        panel[...] = first.T * keep_ref[pl.ds(0, 1), :].astype(jnp.float32)
    load(SLOTS - 1).start()
    lines = [window_sq[:, k : k + LANES] for k in range(0, WINDOW, LANES)]
    own_lines = tile // LANES
    blank = jnp.zeros((STAT - own_lines - len(lines), LANES), jnp.float32)

    def compute(i, dst, stat_dst):
        load(i).wait()
        block = base(steps[i]) // width
        gate = keep_ref[pl.ds(block, 1), :].astype(jnp.float32)
        masked[...] = (panel[...] * gate).astype(jnp.bfloat16)
        squares = []
        for j in range(step // SUB):
            piece = mbuf[i % SLOTS, :, pl.ds(j * SUB, SUB)]
            dst[:, pl.ds(j * SUB, SUB)] = jnp.dot(
                masked[...], piece, preferred_element_type=jnp.float32
            )
            wide = piece.astype(jnp.float32)
            sq = jnp.sum(wide * wide, axis=0, keepdims=True)
            squares += [sq[:, k : k + LANES] for k in range(0, SUB, LANES)]
        for t in range(per):
            mine = squares[t * own_lines : (t + 1) * own_lines]
            stat_dst[:, pl.ds(t * LANES, LANES)] = jnp.concatenate(
                mine + lines + [blank], axis=0
            )
        if i + SLOTS < len(steps):
            load(i + SLOTS).start()

    made = pieces()
    early = [made[n] for n in EARLY]
    first_rows = sum(p.height for p in early)
    ref_of = {key: ref for (key, _), ref in zip(buffers(cfg, tile), bufs)}
    incoming, outgoing = semaphores(cfg)
    twin = device(y, x, 1 - c, z)

    def awaited(ref, sem):
        return pltpu.make_async_remote_copy(
            src_ref=ref, dst_ref=ref, send_sem=sem, recv_sem=sem,
            device_id=twin, device_id_type=MESH,
        )

    def arrived(ref, sem):
        awaited(ref, sem).wait_recv()

    def sent_all(ref, sem):
        awaited(ref, sem).wait_send()

    def array(p):
        return (stat, LANES) if p.stat else (acc, tile)

    def z_copy(p, way, k, t, to):
        src, unit = array(p)
        phase = p.order.index("z")
        g = groups_of(cfg, p.order, phase)[k]
        return pltpu.make_async_remote_copy(
            src_ref=src.at[quad(g), pl.ds(p.start, p.height), pl.ds(t * unit, unit)],
            dst_ref=ref_of[p.name, way].at[t - 1 if way == "up" else t, k],
            send_sem=send_sem.at[outgoing[p.kind, phase]],
            recv_sem=recv_sem.at[incoming[p.name, way, t]],
            device_id=device(y, x, c, to),
            device_id_type=MESH,
        )

    def xy_copies(p, phase, only=None):
        src, unit = array(p)
        axis = p.order[phase]
        kept, sent = exchange(cfg, p.order, phase)
        out = []
        for d in range(len(sent)):
            for k, g in enumerate(sent[d]):
                if "z" in p.order[:phase]:
                    cols = [pl.ds(pl.multiple_of(z * unit, unit), unit)]
                elif phase == 0 and p in early:
                    part = Z * unit // halves
                    cols = [pl.ds(h * part, part) for h in range(halves)]
                else:
                    cols = [pl.ds(0, Z * unit)]
                for h, part in enumerate(cols):
                    if only is not None and only != (g, h):
                        continue
                    dst = ref_of[p.name, phase].at[d, k]
                    if len(cols) > 1:
                        dst = ref_of[p.name, phase].at[d, k, :, part]
                    out.append(
                        pltpu.make_async_remote_copy(
                            src_ref=src.at[quad(g), pl.ds(p.start, p.height), part],
                            dst_ref=dst,
                            send_sem=send_sem.at[outgoing[p.kind, phase]],
                            recv_sem=recv_sem.at[incoming[p.name, phase]],
                            device_id=peer(axis, d + 1),
                            device_id_type=MESH,
                        )
                    )
        return out

    def z_stage(p, s):
        src, unit = array(p)
        phase = p.order.index("z")
        here = groups_of(cfg, p.order, phase)

        def take(way, t):
            ref = ref_of[p.name, way].at[t - 1 if way == "up" else t]
            arrived(ref, recv_sem.at[incoming[p.name, way, t]])
            for k, g in enumerate(here):
                where = (quad(g), pl.ds(p.start, p.height), pl.ds(t * unit, unit))
                src[where] += ref[k]

        @pl.when(z == s)
        def _():
            for t in reversed(range(s, Z)):
                if s > 0:
                    take("up", t)
                if t > s:
                    for k in range(len(here)):
                        z_copy(p, "up", k, t, s + 1).start()

        top = Z - 1 - s

        @pl.when(z == top)
        def _():
            for t in range(top + 1):
                if s > 0:
                    take("down", t)
                if t < top:
                    for k in range(len(here)):
                        z_copy(p, "down", k, t, top - 1).start()

    def begin(p, phase):
        if phase < len(p.order) and p.order[phase] != "z":
            for copy in xy_copies(p, phase):
                copy.start()

    def finish(p, phase):
        src, unit = array(p)
        kept, sent = exchange(cfg, p.order, phase)
        if not sent:
            return
        ref = ref_of[p.name, phase]
        arrived(ref, recv_sem.at[incoming[p.name, phase]])
        if "z" in p.order[:phase]:
            cols = pl.ds(pl.multiple_of(z * unit, unit), unit)
        else:
            cols = pl.ds(0, Z * unit)
        for k, g in enumerate(kept):
            where = (quad(g), pl.ds(p.start, p.height), cols)
            total = src[where]
            for d in range(len(sent)):
                total = total + ref[d, k]
            src[where] = total

    cuts = ((0, first_rows), (first_rows, WINDOW - first_rows))

    def to_sibling(n, part):
        if part < 2:
            where = (n, pl.ds(*cuts[part]))
            src, dst = sib_out.at[where], sib_in.at[where]
            number = part * len(units) + n
        else:
            src, dst = stat_out.at[n], stat_in.at[n]
            number = 2 * len(units)
        pltpu.make_async_remote_copy(
            src_ref=src,
            dst_ref=dst,
            send_sem=sib_send.at[part],
            recv_sem=sib_recv.at[number],
            device_id=twin,
            device_id_type=MESH,
        ).start()

    def first_sends(p, g, h):
        if p.order[0] != "z":
            for copy in xy_copies(p, 0, (g, h)):
                copy.start()
            return
        k = groups_of(cfg, p.order, 0).index(g)
        tiles = range(h * per, (h + 1) * per)

        @pl.when(z == 0)
        def _():
            for t in reversed(tiles):
                if t > 0:
                    z_copy(p, "up", k, t, 1).start()

        @pl.when(z == Z - 1)
        def _():
            for t in tiles:
                if t < Z - 1:
                    z_copy(p, "down", k, t, Z - 2).start()

    def merge(n, part):
        g, h = units[n]
        q = quad(g)
        low, size = cuts[part]
        where = (n, pl.ds(low, size))
        arrived(sib_in.at[where], sib_recv.at[part * len(units) + n])

        def add(j, carry):
            at = pl.multiple_of(j * 8, 8)
            acc[q, pl.ds(at, 8), pl.ds(h * step, step)] += sib_in[n, pl.ds(at, 8), :]
            return carry

        lax.fori_loop(low // 8, (low + size) // 8, add, 0)
        if part == 0:
            for p in early:
                first_sends(p, g, h)

    def merge_stat():
        arrived(stat_in, sib_recv.at[2 * len(units)])
        for n, (g, h) in enumerate(units):
            stat[quad(g), :, pl.ds(h * per * LANES, per * LANES)] += stat_in[n]

    last = len(units) - 1
    for n, (g, h) in enumerate(units):
        with scope(f"a{n}"):
            compute(2 * n, sib_out.at[n], stat_out.at[n])
        if n == 0:
            with scope("barrier"):
                await_peers()
        to_sibling(n, 0)
        if n:
            to_sibling(n - 1, 1)
            to_sibling(n - 1, 2)
            with scope(f"m{n - 1}"):
                merge(n - 1, 0)
        with scope(f"b{n}"):
            compute(
                2 * n + 1,
                acc.at[quad(g), :, pl.ds(h * step, step)],
                stat.at[quad(g), :, pl.ds(h * per * LANES, per * LANES)],
            )
    to_sibling(last, 1)
    to_sibling(last, 2)
    with scope(f"m{last}"):
        merge(last, 0)

    def stages(s):
        return range(-(-s * Z // STAGES), -(-(s + 1) * Z // STAGES))

    def rest(n):
        return range(n * len(units) // RESTS, (n + 1) * len(units) // RESTS)

    for op in ORDER:
        if op[0] == "R":
            with scope(f"R{op[2]}"):
                for n in rest(op[2]):
                    merge(n, 1)
                    if n == last:
                        merge_stat()
            continue
        p = made[op[1]]
        if op[0] == "S":
            begin(p, 0)
        elif op[0] == "F":
            with scope(f"F{op[1]}.{op[2]}"):
                finish(p, op[2])
                begin(p, op[2] + 1)
        else:
            with scope(f"Z{op[1]}.{op[2]}"):
                for s in stages(op[2]):
                    if s > 0 or p not in early or p.order[0] != "z":
                        z_stage(p, s)
                if op[2] == STAGES - 1:
                    begin(p, p.order.index("z") + 1)

    with scope("final"):
        own = y * X + x
        tail = stat[own, :, pl.ds(pl.multiple_of(z * LANES, LANES), LANES)]
        tail = 1.0 / jnp.sqrt(tail + 1e-06)
        scale = jnp.concatenate([tail[k : k + 1] for k in range(own_lines)], axis=1)
        win = jnp.concatenate(
            [tail[own_lines + k : own_lines + k + 1] for k in range(len(lines))], axis=1
        )
        mine = acc[own, :, pl.ds(pl.multiple_of(z * tile, tile), tile)]
        out_ref[...] = (mine * scale).T * win

    with scope("drain"):
        for part in range(2):
            sent_all(sib_out.at[:, pl.ds(*cuts[part])], sib_send.at[part])
        sent_all(stat_out, sib_send.at[2])
        for (kind, phase), n in outgoing.items():
            same = [p for p in made.values() if p.kind == kind]
            src, unit = array(same[0])
            order = same[0].order
            if order[phase] == "z":
                count, cols = len(groups_of(cfg, order, phase)), (Z - 1) * unit
            else:
                kept, sent = exchange(cfg, order, phase)
                count = len(kept) * len(sent)
                cols = unit if "z" in order[:phase] else Z * unit
            high = sum(p.height for p in same)
            if count and cols:
                all_sent = src.at[pl.ds(0, count), pl.ds(0, high), pl.ds(0, cols)]
                sent_all(all_sent, send_sem.at[n])


def shards(matrix, keep_mask):
    depth, columns = matrix.shape
    blocks = keep_mask.shape[0]
    width = columns // blocks
    outer = lax.axis_size("rows")
    inner = lax.axis_size("grp")
    tile = columns // (outer * inner)
    span = inner * tile
    step = min(width, span)
    cfg = {"x": 2, "y": outer // 4, "z": inner, "tile": tile, "width": width}
    cfg["step"] = step
    quads = cfg["x"] * cfg["y"]
    links = quads * (span // step)
    recv, send = semaphores(cfg)
    flat = step // tile * LANES
    return pl.pallas_call(
        functools.partial(kernel, cfg),
        out_shape=jax.ShapeDtypeStruct((tile, WINDOW), jnp.float32),
        in_specs=[
            pl.BlockSpec(memory_space=pltpu.HBM),
            pl.BlockSpec(memory_space=pltpu.HBM),
        ],
        out_specs=pl.BlockSpec(memory_space=pltpu.VMEM),
        scratch_shapes=[
            pltpu.VMEM((quads, WINDOW, span), jnp.float32),
            pltpu.VMEM((quads, STAT, inner * LANES), jnp.float32),
            pltpu.VMEM((links, WINDOW, step), jnp.float32),
            pltpu.VMEM((links, WINDOW, step), jnp.float32),
            pltpu.VMEM((links, STAT, flat), jnp.float32),
            pltpu.VMEM((links, STAT, flat), jnp.float32),
            pltpu.VMEM((SLOTS, depth, step), jnp.bfloat16),
            pltpu.VMEM(keep_mask.shape, keep_mask.dtype),
            pltpu.VMEM((WINDOW, depth), jnp.float32),
            pltpu.VMEM((WINDOW, depth), jnp.bfloat16),
            pltpu.SemaphoreType.DMA((SLOTS,)),
            pltpu.SemaphoreType.DMA,
            pltpu.SemaphoreType.DMA((3,)),
            pltpu.SemaphoreType.DMA((2 * links + 1,)),
            pltpu.SemaphoreType.DMA((len(send),)),
            pltpu.SemaphoreType.DMA((len(recv),)),
        ]
        + [pltpu.VMEM(shape, jnp.float32) for _, shape in buffers(cfg, tile)],
        compiler_params=pltpu.CompilerParams(
            collective_id=0, has_side_effects=True, vmem_limit_bytes=LIMIT * 1024 * 1024
        ),
        cost_estimate=pl.CostEstimate(
            flops=2 * depth * columns * WINDOW,
            bytes_accessed=2 * depth * columns,
            transcendentals=0,
        ),
    )(matrix, pltpu.with_memory_space_constraint(keep_mask, pltpu.HBM))


def solution(mesh):
    in_specs = (P(("rows", "grp"), None), P(None, ("rows", "grp")))
    out_specs = P(("rows", "grp"), None)
    return jax.shard_map(
        shards, mesh=mesh, in_specs=in_specs, out_specs=out_specs, check_vma=False
    )
```

time: 90.7 us -> 78.8 us (0.87)
  Pallas kernels: 88.6 us -> 77.9 us
  local copies, waits for them, and re-layouts: 1.87 us -> 0.8 us
    pallas_call x1, Pallas kernels: 88.6 us -> 77.9 us  [shards(): pl.pallas_call(functools.partial(kernel, cfg), out_shape=jax.ShapeDtypeSt...]
    unnamed x1, local copies, waits for them, and re-layouts: 1.87 us -> 0.8 us
where the time goes in v1:
time: 78.8 us; the launch traced here: 78.7 us
  Pallas kernels  77.9 us (99%)
  local copies, waits for them, and re-layouts  0.8 us (1%)
    pallas_call x1, Pallas kernels, shards(): pl.pallas_call(functools.partial(kernel, cfg), out_shape=jax.ShapeDtypeSt...  77.9 us

profile of v1, /device:TPU:0, one launch (start us, length us, event | category | flops | bytes accessed | tf_op | source)
XLA Modules:
  0.0 78.7 jit_solution(17659230370095631068)
XLA Ops:
  0.0 77.9 %shard_map.28 = f32[512,256]{1,0:T(8,128)S(1)} custom-call(bf16[768,16384]{1,0:T(8,128)(2,1)} %matrix_ref.1, s32[16,768]{1,0:T(8,128)} %keep_hbm.1), custom_call_target="tpu_custom_call" | custom-call | flops 6442450944 | bytes 25165824 | tf_op jit(solution)/shard_map/pallas_call | solution.py:621
  77.9 0.8 %copy.4 = f32[512,256]{1,0:T(8,128)} copy(f32[512,256]{1,0:T(8,128)S(1)} %shard_map.28) | data formatting | bytes 1048576

commit v2 on v1

v2 whole, which is shorter than its diff:
```python
import contextlib
import functools

import jax
import jax.numpy as jnp
from jax import lax
from jax.experimental import pallas as pl
from jax.experimental.pallas import tpu as pltpu
from jax.sharding import PartitionSpec as P

WINDOW = 256
LANES = 128
STAT = 8
SUB = 256
SLOTS = 4
MESH = pl.DeviceIdType.MESH
KINDS = {
    "A": "xypq", "B": "yxpq", "C": "pqxy", "D": "pqyx", "E": "xpyq", "F": "ypxq",
    "G": "pxyq", "H": "pyxq", "I": "pxqy", "J": "pyqx", "K": "xpqy", "L": "ypqx",
}
HEIGHTS = (
    ("E0", 16),
    ("D1", 8),
    ("B0", 32),
    ("B3", 16),
    ("C0", 16),
    ("D0", 16),
    ("C1", 16),
    ("A0", 40),
    ("B1", 24),
    ("A1", 16),
    ("B2", 16),
    ("A2", 16),
    ("B4", 8),
    ("A3", 8),
    ("B5", 8),
)
EARLY = ("E0", "D1", "B0", "B3", "C0", "D0", "C1", "A0", )
STAT_KIND = "F"
LIMIT = 50
ORDER = (
    ("R", "R", 0),
    ("S", "B1", 0),
    ("F", "B0", 0),
    ("F", "C0", 0),
    ("F", "E0", 0),
    ("F", "D0", 0),
    ("S", "A1", 0),
    ("F", "A0", 0),
    ("F", "B0", 1),
    ("F", "B1", 0),
    ("F", "C1", 0),
    ("S", "B2", 0),
    ("F", "A1", 0),
    ("F", "A0", 1),
    ("S", "A2", 0),
    ("S", "T", 0),
    ("F", "D1", 0),
    ("F", "B1", 1),
    ("F", "B2", 0),
    ("S", "B5", 0),
    ("F", "B0", 2),
    ("S", "B4", 0),
    ("F", "A1", 1),
    ("F", "B3", 0),
    ("F", "A2", 0),
    ("S", "A3", 0),
    ("F", "C1", 1),
    ("F", "T", 0),
    ("F", "E0", 1),
    ("F", "A0", 2),
    ("F", "B5", 0),
    ("F", "B2", 1),
    ("F", "B1", 2),
    ("F", "D1", 1),
    ("F", "C0", 1),
    ("F", "B3", 1),
    ("F", "A1", 2),
    ("F", "A3", 0),
    ("F", "B0", 3),
    ("F", "T", 1),
    ("F", "B4", 0),
    ("F", "A2", 1),
    ("F", "D0", 1),
    ("F", "C1", 2),
    ("F", "E0", 2),
    ("F", "B5", 1),
    ("F", "D1", 2),
    ("F", "B2", 2),
    ("F", "C0", 2),
    ("F", "A3", 1),
    ("F", "B3", 2),
    ("F", "D0", 2),
    ("F", "B4", 1),
    ("F", "A2", 2),
    ("F", "B5", 2),
    ("F", "T", 2),
    ("F", "B2", 3),
    ("F", "A3", 2),
    ("F", "B1", 3),
    ("F", "C0", 3),
    ("F", "A0", 3),
    ("F", "B4", 2),
    ("F", "D1", 3),
    ("F", "T", 3),
    ("F", "E0", 3),
    ("F", "A2", 3),
    ("F", "A3", 3),
    ("F", "C1", 3),
    ("F", "D0", 3),
    ("F", "B5", 3),
    ("F", "A1", 3),
    ("F", "B3", 3),
    ("F", "B4", 3),
)


def scope(name):
    return contextlib.nullcontext()


class Piece:
    def __init__(self, name, start, height, order, stat):
        self.name, self.start, self.height = name, start, height
        self.order, self.stat, self.kind = order, stat, name[0]


def bits_of(sizes):
    bits = sizes["z"].bit_length() - 1
    assert sizes["z"] == 1 << bits and bits <= 3
    return "pqr"[:bits]


def reversed_of(t, bits):
    return sum(((t >> k) & 1) << (bits - 1 - k) for k in range(bits))


def block_offsets(cfg):
    per, bits = cfg["step"] // cfg["tile"], len(bits_of(cfg))
    out = []
    for j in range(per):
        found = {
            reversed_of(low + j, bits) * cfg["tile"] // cfg["width"]
            for low in range(0, cfg["z"], per)
        }
        assert len(found) == 1
        out.append(found.pop())
    return out


def axes_of(sizes, kind):
    order = ""
    for axis in KINDS[kind]:
        order += axis
        if axis == "q":
            order += "r"
    return "".join(a for a in order if a in "xy" or a in bits_of(sizes))


def pieces(sizes):
    out, at = {}, 0
    for name, height in HEIGHTS:
        out[name] = Piece(name, at, height, axes_of(sizes, name[0]), False)
        at += height
    assert at == WINDOW
    out["T"] = Piece("T", 0, STAT, axes_of(sizes, STAT_KIND), True)
    return out


def held(sizes, order, phase):
    fixed = order[:phase]
    return [
        (dx, dy)
        for dx in reversed(range(sizes["x"]))
        for dy in reversed(range(sizes["y"]))
        if not ("x" in fixed and dx) and not ("y" in fixed and dy)
    ]


def exchange(sizes, order, phase):
    axis = order[phase]
    quads = held(sizes, order, phase)
    if axis not in "xy":
        return quads, [quads]
    i = "xy".index(axis)
    kept = [g for g in quads if g[i] == 0]
    sent = [
        [(d, g[1]) if axis == "x" else (g[0], d) for g in kept]
        for d in range(1, sizes[axis])
    ]
    return kept, sent


def slots_of(sizes, order, phase):
    done = sum(a not in "xy" for a in order[: phase + 1])
    return sizes["z"] >> done


def tiles_sent(sizes, order, phase):
    kept, sent = exchange(sizes, order, phase)
    return len(kept) * len(sent) * slots_of(sizes, order, phase)


def buffers(sizes, tile):
    out = []
    for p in pieces(sizes).values():
        unit = LANES if p.stat else tile
        for phase in range(len(p.order)):
            kept, sent = exchange(sizes, p.order, phase)
            cols = slots_of(sizes, p.order, phase) * unit
            shape = (max(1, len(sent)), len(kept), p.height, cols)
            out.append(((p.name, phase), shape))
    return out


def semaphores(sizes):
    recv, send = {}, {}
    for p in pieces(sizes).values():
        for phase in range(len(p.order)):
            send.setdefault((p.stat, tiles_sent(sizes, p.order, phase)), len(send))
            recv[p.name, phase] = len(recv)
    return recv, send


def kernel(cfg, matrix_ref, keep_hbm, out_ref, acc, stat, sib_out, sib_in, stat_out,
           stat_in, mbuf, keep_ref, panel, masked, load_sem, keep_sem, sib_send,
           sib_recv, send_sem, recv_sem, line_sem, *bufs):
    X, Y, Z, tile, width, step = (
        cfg["x"], cfg["y"], cfg["z"], cfg["tile"], cfg["width"], cfg["step"]
    )
    span = Z * tile
    halves = span // step
    per = step // tile
    rows = lax.axis_index("rows")
    z = lax.axis_index("grp")
    c = lax.rem(rows, 2)
    x = lax.rem(rows // 2, X)
    y = rows // (2 * X)

    def device(yy, xx, cc, zz):
        return ((yy * X + xx) * 2 + cc, zz)

    def quad(g):
        return lax.rem(y + g[1], Y) * X + lax.rem(x + g[0], X)

    def bit(axis):
        return lax.rem(z // (1 << "pqr".index(axis)), 2)

    def peer(axis, d):
        if axis == "x":
            return device(y, lax.rem(x + d, X), c, z)
        if axis == "y":
            return device(lax.rem(y + d, Y), x, c, z)
        return device(y, x, c, z + (1 << "pqr".index(axis)) * (1 - 2 * bit(axis)))

    short = Z <= 4
    peers = [device(y, x, 1 - c, z)]
    for axis, n in [("x", X), ("y", Y)] + [(b, 2) for b in bits_of(cfg) if not short]:
        peers += [peer(axis, d) for d in range(1, n)]
    below, above = jnp.where(z > 0, 1, 0), jnp.where(z < Z - 1, 1, 0)

    def tell(sem, device_id):
        pl.semaphore_signal(sem, inc=1, device_id=device_id, device_id_type=MESH)

    def tell_line(sem):
        @pl.when(z > 0)
        def _():
            tell(sem, device(y, x, c, z - 1))

        @pl.when(z < Z - 1)
        def _():
            tell(sem, device(y, x, c, z + 1))

    barrier = pltpu.get_barrier_semaphore()
    for p in peers:
        tell(barrier, p)
    if short:
        tell_line(barrier)

    def await_peers():
        pl.semaphore_wait(barrier, len(peers) + (below + above if short else 0))
        if short:
            tell_line(line_sem)

    names = bits_of(cfg)

    def reversed_bits(t):
        return reversed_of(t, len(names))

    groups = [(dx, dy) for dx in reversed(range(X)) for dy in reversed(range(Y))]
    units = [(groups[0], h) for h in range(halves)]
    units += [(g, h) for h in range(halves) for g in groups[1:-1]]
    units += [(groups[-1], h) for h in range(halves)]
    steps = [(g, own, h) for g, h in units for own in (0, 1)]

    def half(h):
        if halves != 2:
            return h
        return 1 - bit("p") if h == 0 else bit("p")

    def span_of(h, size):
        return pl.ds(pl.multiple_of(half(h) * size, size), size)

    def base(s):
        g, own, h = s
        cc = c if own else 1 - c
        return pl.multiple_of((quad(g) * 2 + cc) * span, span)

    def load(i):
        first, h = base(steps[i]), steps[i][2]
        for j in range(per):
            t = reversed_bits(half(h) * per + j)
            pltpu.make_async_copy(
                matrix_ref.at[:, pl.ds(pl.multiple_of(first + t * tile, tile), tile)],
                mbuf.at[i % SLOTS, :, pl.ds(j * tile, tile)],
                load_sem.at[i % SLOTS],
            ).start()

    def loaded(i):
        pltpu.make_async_copy(
            matrix_ref.at[:, pl.ds(0, step)], mbuf.at[i % SLOTS], load_sem.at[i % SLOTS]
        ).wait()

    window = pltpu.make_async_copy(
        matrix_ref.at[:, pl.ds(0, WINDOW)],
        mbuf.at[SLOTS - 1, :, pl.ds(0, WINDOW)],
        load_sem.at[SLOTS - 1],
    )
    keep = pltpu.make_async_copy(keep_hbm, keep_ref, keep_sem)
    window.start()
    keep.start()
    load(0)

    with scope("head"):
        window.wait()
        load(1)
        keep.wait()
        first = mbuf[SLOTS - 1, :, pl.ds(0, WINDOW)].astype(jnp.float32)
        window_sq = jnp.sum(first * first, axis=0, keepdims=True)
        panel[...] = first.T * keep_ref[pl.ds(0, 1), :].astype(jnp.float32)
    for i in range(2, SLOTS):
        load(i)
    lines = [window_sq[:, k : k + LANES] for k in range(0, WINDOW, LANES)]
    own_lines = tile // LANES
    blank = jnp.zeros((STAT - own_lines - len(lines), LANES), jnp.float32)

    offsets = block_offsets(cfg)
    kinds = sorted(set(offsets))

    def compute(i, dst, stat_dst):
        loaded(i)
        g, own, h = steps[i]
        at = (groups.index(g) * 2 + own) * len(kinds)
        if h == 0:
            for k, offset in enumerate(kinds):
                block = base(steps[i]) // width + offset
                gate = keep_ref[pl.ds(block, 1), :].astype(jnp.float32)
                masked[at + k] = (panel[...] * gate).astype(jnp.bfloat16)
        squares = []
        for j in range(step // SUB):
            piece = mbuf[i % SLOTS, :, pl.ds(j * SUB, SUB)]
            dst[:, pl.ds(j * SUB, SUB)] = jnp.dot(
                masked[at + kinds.index(offsets[j * SUB // tile])],
                piece,
                preferred_element_type=jnp.float32,
            )
            wide = piece.astype(jnp.float32)
            sq = jnp.sum(wide * wide, axis=0, keepdims=True)
            squares += [sq[:, k : k + LANES] for k in range(0, SUB, LANES)]
        for t in range(per):
            mine = squares[t * own_lines : (t + 1) * own_lines]
            stat_dst[:, pl.ds(t * LANES, LANES)] = jnp.concatenate(
                mine + lines + [blank], axis=0
            )
        if i + SLOTS < len(steps):
            load(i + SLOTS)

    made = pieces(cfg)
    early = [made[n] for n in EARLY]
    first_rows = sum(p.height for p in early)
    ref_of = {key: ref for (key, _), ref in zip(buffers(cfg, tile), bufs)}
    incoming, outgoing = semaphores(cfg)
    twin = device(y, x, 1 - c, z)

    def awaited(ref, sem):
        return pltpu.make_async_remote_copy(
            src_ref=ref, dst_ref=ref, send_sem=sem, recv_sem=sem,
            device_id=twin, device_id_type=MESH,
        )

    def arrived(ref, sem):
        awaited(ref, sem).wait_recv()

    def sent_all(ref, sem):
        awaited(ref, sem).wait_send()

    def array(p):
        return (stat, LANES) if p.stat else (acc, tile)

    def columns(p, phase, away):
        unit = array(p)[1]
        low = 0
        for axis in p.order[:phase]:
            if axis not in "xy":
                low += bit(axis) * (Z >> (names.index(axis) + 1))
        axis = p.order[phase]
        count = slots_of(cfg, p.order, phase)
        if axis not in "xy":
            low += (1 - bit(axis) if away else bit(axis)) * count
        if isinstance(low, int):
            return pl.ds(low * unit, count * unit)
        return pl.ds(pl.multiple_of(low * unit, unit), count * unit)

    def copy(p, phase, d, k, g, cols, part=None):
        src = array(p)[0]
        dst = ref_of[p.name, phase].at[d, k]
        if part is not None:
            dst = ref_of[p.name, phase].at[d, k, :, part]
        return pltpu.make_async_remote_copy(
            src_ref=src.at[quad(g), pl.ds(p.start, p.height), cols],
            dst_ref=dst,
            send_sem=send_sem.at[outgoing[p.stat, tiles_sent(cfg, p.order, phase)]],
            recv_sem=recv_sem.at[incoming[p.name, phase]],
            device_id=peer(p.order[phase], d + 1),
            device_id_type=MESH,
        )

    def begin(p, phase):
        if phase < len(p.order):
            cols = columns(p, phase, True)
            for d, quads in enumerate(exchange(cfg, p.order, phase)[1]):
                for k, g in enumerate(quads):
                    copy(p, phase, d, k, g, cols).start()

    def finish(p, phase):
        src = array(p)[0]
        kept, sent = exchange(cfg, p.order, phase)
        if not sent:
            return
        ref = ref_of[p.name, phase]
        arrived(ref, recv_sem.at[incoming[p.name, phase]])
        cols = columns(p, phase, False)
        for k, g in enumerate(kept):
            where = (quad(g), pl.ds(p.start, p.height), cols)
            total = src[where]
            for d in range(len(sent)):
                total = total + ref[d, k]
            src[where] = total

    links = []
    for p in early:
        links += [] if p.order[0] in [q.order[0] for q in links] else [p]
    head_rows = sum(p.height for p in links)
    ahead, behind, whole, later = (
        (0, head_rows),
        (head_rows, first_rows - head_rows),
        (0, first_rows),
        (first_rows, WINDOW - first_rows),
    )
    assert early[: len(links)] == links
    last = len(units) - 1

    def to_sibling(n, rows, number):
        if rows:
            where = (n, pl.ds(*rows))
            src, dst = sib_out.at[where], sib_in.at[where]
            kind = 1 if rows == later else 0
        else:
            src, dst, kind = stat_out.at[n], stat_in.at[n], 2
        pltpu.make_async_remote_copy(
            src_ref=src,
            dst_ref=dst,
            send_sem=sib_send.at[kind],
            recv_sem=sib_recv.at[number],
            device_id=twin,
            device_id_type=MESH,
        ).start()

    def offer(n):
        if n == 0 and behind[1]:
            to_sibling(0, ahead, 0)
            to_sibling(0, behind, last + 1)
        else:
            to_sibling(n, whole, n)

    def offer_rest(n):
        to_sibling(n, later, last + 2)
        to_sibling(n, None, last + 3)

    def first_sends(p, g, h):
        axis = p.order[0]
        for d, quads in enumerate(exchange(cfg, p.order, 0)[1]):
            if g not in quads:
                continue
            k = quads.index(g)
            if axis in "xy":
                part = span_of(h, step)
                copy(p, 0, d, k, g, part, part if halves > 1 else None).start()
            elif halves == 1:
                copy(p, 0, d, k, g, columns(p, 0, True)).start()
            elif halves == 2:
                if h == 0:
                    copy(p, 0, d, k, g, span_of(h, step)).start()
            else:

                @pl.when(bit(axis) == 1 - 2 * h // halves)
                def _():
                    part = pl.ds(h * step % (span // 2), step)
                    copy(p, 0, d, k, g, pl.ds(h * step, step), part).start()

    def add_rows(n, rows):
        g, h = units[n]
        q = quad(g)
        low, size = rows
        cols = span_of(h, step)

        def add(j, carry):
            at = pl.multiple_of(j * 8, 8)
            acc[q, pl.ds(at, 8), cols] += sib_in[n, pl.ds(at, 8), :]
            return carry

        lax.fori_loop(low // 8, (low + size) // 8, add, 0)
        for p in early:
            if low <= p.start < low + size:
                first_sends(p, g, h)

    def merge(n):
        parts = [(whole, n)]
        if n == 0 and behind[1]:
            parts = [(ahead, 0), (behind, last + 1)]
        for rows, number in parts:
            arrived(sib_in.at[n, pl.ds(*rows)], sib_recv.at[number])
            add_rows(n, rows)

    def merge_rest():
        arrived(sib_in.at[:, pl.ds(*later)], sib_recv.at[last + 2])
        for n in range(len(units)):
            add_rows(n, later)
        arrived(stat_in, sib_recv.at[last + 3])
        for n, (g, h) in enumerate(units):
            stat[quad(g), :, span_of(h, per * LANES)] += stat_in[n]

    for n, (g, h) in enumerate(units):
        with scope(f"a{n}"):
            compute(2 * n, sib_out.at[n], stat_out.at[n])
        if n == 0:
            with scope("barrier"):
                await_peers()
        offer(n)
        if n:
            offer_rest(n - 1)
        if n > 1:
            with scope(f"m{n - 1}"):
                merge(n - 1)
        with scope(f"b{n}"):
            compute(
                2 * n + 1,
                acc.at[quad(g), :, span_of(h, step)],
                stat.at[quad(g), :, span_of(h, per * LANES)],
            )
        if n == 0:
            with scope("m0"):
                merge(0)
    offer_rest(last)
    if last:
        with scope(f"m{last}"):
            merge(last)

    for op in ORDER:
        if op[0] == "R":
            if short:
                pl.semaphore_wait(line_sem, below + above)
            with scope("R"):
                merge_rest()
            continue
        p = made[op[1]]
        if op[0] == "S":
            begin(p, 0)
        elif op[2] < len(p.order):
            with scope(f"F{op[1]}.{op[2]}"):
                finish(p, op[2])
                begin(p, op[2] + 1)
    for p in made.values():
        for phase in range(4, len(p.order)):
            finish(p, phase)
            begin(p, phase + 1)

    with scope("final"):
        own = y * X + x
        slot = sum(bit(b) * (Z >> (k + 1)) for k, b in enumerate(names))
        tail = stat[own, :, pl.ds(pl.multiple_of(slot * LANES, LANES), LANES)]
        tail = 1.0 / jnp.sqrt(tail + 1e-06)
        scale = jnp.concatenate([tail[k : k + 1] for k in range(own_lines)], axis=1)
        win = jnp.concatenate(
            [tail[own_lines + k : own_lines + k + 1] for k in range(len(lines))], axis=1
        )
        mine = acc[own, :, pl.ds(pl.multiple_of(slot * tile, tile), tile)]
        out_ref[...] = (mine * scale).T * win

    with scope("drain"):
        sent_all(sib_out.at[:, pl.ds(*whole)], sib_send.at[0])
        sent_all(sib_out.at[:, pl.ds(*later)], sib_send.at[1])
        sent_all(stat_out, sib_send.at[2])
        for (is_stat, tiles), n in outgoing.items():
            high = sum(
                p.height
                for p in made.values()
                for phase in range(len(p.order))
                if p.stat == is_stat and tiles_sent(cfg, p.order, phase) == tiles
            )
            if tiles:
                src, unit = (stat, LANES) if is_stat else (acc, tile)
                wide = max(w for w in range(1, Z + 1) if tiles % w == 0)
                same = src.at[
                    pl.ds(0, tiles // wide), pl.ds(0, high), pl.ds(0, wide * unit)
                ]
                sent_all(same, send_sem.at[n])


def shards(matrix, keep_mask):
    depth, columns = matrix.shape
    blocks = keep_mask.shape[0]
    width = columns // blocks
    outer = lax.axis_size("rows")
    inner = lax.axis_size("grp")
    tile = columns // (outer * inner)
    span = inner * tile
    step = min(width, span)
    cfg = {"x": 2, "y": outer // 4, "z": inner, "tile": tile, "width": width}
    cfg["step"] = step
    quads = cfg["x"] * cfg["y"]
    links = quads * (span // step)
    recv, send = semaphores(cfg)
    flat = step // tile * LANES
    return pl.pallas_call(
        functools.partial(kernel, cfg),
        out_shape=jax.ShapeDtypeStruct((tile, WINDOW), jnp.float32),
        in_specs=[
            pl.BlockSpec(memory_space=pltpu.HBM),
            pl.BlockSpec(memory_space=pltpu.HBM),
        ],
        out_specs=pl.BlockSpec(memory_space=pltpu.VMEM),
        scratch_shapes=[
            pltpu.VMEM((quads, WINDOW, span), jnp.float32),
            pltpu.VMEM((quads, STAT, inner * LANES), jnp.float32),
            pltpu.VMEM((links, WINDOW, step), jnp.float32),
            pltpu.VMEM((links, WINDOW, step), jnp.float32),
            pltpu.VMEM((links, STAT, flat), jnp.float32),
            pltpu.VMEM((links, STAT, flat), jnp.float32),
            pltpu.VMEM((SLOTS, depth, step), jnp.bfloat16),
            pltpu.VMEM(keep_mask.shape, keep_mask.dtype),
            pltpu.VMEM((WINDOW, depth), jnp.float32),
            pltpu.VMEM((2 * quads * len(set(block_offsets(cfg))), WINDOW, depth), jnp.bfloat16),
            pltpu.SemaphoreType.DMA((SLOTS,)),
            pltpu.SemaphoreType.DMA,
            pltpu.SemaphoreType.DMA((3,)),
            pltpu.SemaphoreType.DMA((links + 3,)),
            pltpu.SemaphoreType.DMA((len(send),)),
            pltpu.SemaphoreType.DMA((len(recv),)),
            pltpu.SemaphoreType.REGULAR,
        ]
        + [pltpu.VMEM(shape, jnp.float32) for _, shape in buffers(cfg, tile)],
        compiler_params=pltpu.CompilerParams(
            collective_id=0, has_side_effects=True, vmem_limit_bytes=LIMIT * 1024 * 1024
        ),
        cost_estimate=pl.CostEstimate(
            flops=2 * depth * columns * WINDOW,
            bytes_accessed=2 * depth * columns,
            transcendentals=0,
        ),
    )(matrix, pltpu.with_memory_space_constraint(keep_mask, pltpu.HBM))


def solution(mesh):
    in_specs = (P(("rows", "grp"), None), P(None, ("rows", "grp")))
    out_specs = P(("rows", "grp"), None)
    return jax.shard_map(
        shards, mesh=mesh, in_specs=in_specs, out_specs=out_specs, check_vma=False
    )
```

time: 78.8 us -> 72.8 us (0.924)
  Pallas kernels: 77.9 us -> 71.8 us
    pallas_call x1, Pallas kernels: 77.9 us -> 71.8 us  [shards(): pl.pallas_call(functools.partial(kernel, cfg), out_shape=jax.ShapeDtypeSt...]
where the time goes in v2:
time: 72.8 us; the launch traced here: 72.7 us
  Pallas kernels  71.8 us (99%)
  local copies, waits for them, and re-layouts  0.8 us (1%)
    pallas_call x1, Pallas kernels, shards(): pl.pallas_call(functools.partial(kernel, cfg), out_shape=jax.ShapeDtypeSt...  71.8 us

profile of v2, /device:TPU:0, one launch (start us, length us, event | category | flops | bytes accessed | tf_op | source)
XLA Modules:
  0.0 72.7 jit_solution(8938525797155923701)
XLA Ops:
  0.0 71.8 %shard_map.28 = f32[512,256]{1,0:T(8,128)S(1)} custom-call(bf16[768,16384]{1,0:T(8,128)(2,1)} %matrix_ref.1, s32[16,768]{1,0:T(8,128)} %keep_hbm.1), custom_call_target="tpu_custom_call" | custom-call | flops 6442450944 | bytes 25165824 | tf_op jit(solution)/shard_map/pallas_call | solution.py:635
  71.9 0.8 %copy.4 = f32[512,256]{1,0:T(8,128)} copy(f32[512,256]{1,0:T(8,128)S(1)} %shard_map.28) | data formatting | bytes 1048576

commit v3 on v2

--- a/solution.py
+++ b/solution.py
@@ -13,104 +13,145 @@
 STAT = 8
 SUB = 256
 SLOTS = 4
+PHASES = 4
 MESH = pl.DeviceIdType.MESH
 KINDS = {
     "A": "xypq", "B": "yxpq", "C": "pqxy", "D": "pqyx", "E": "xpyq", "F": "ypxq",
     "G": "pxyq", "H": "pyxq", "I": "pxqy", "J": "pyqx", "K": "xpqy", "L": "ypqx",
 }
 HEIGHTS = (
+    ("C0", 16),
+    ("B3", 8),
     ("E0", 16),
-    ("D1", 8),
-    ("B0", 32),
-    ("B3", 16),
-    ("C0", 16),
+    ("D1", 16),
+    ("B0", 40),
     ("D0", 16),
-    ("C1", 16),
-    ("A0", 40),
-    ("B1", 24),
-    ("A1", 16),
+    ("A1", 32),
+    ("A0", 16),
+    ("B1", 32),
+    ("E1", 16),
     ("B2", 16),
+    ("B4", 8),
+    ("B5", 8),
     ("A2", 16),
-    ("B4", 8),
-    ("A3", 8),
-    ("B5", 8),
 )
-EARLY = ("E0", "D1", "B0", "B3", "C0", "D0", "C1", "A0", )
-STAT_KIND = "F"
+EARLY = ("C0", "B3", "E0", "D1", "B0", "D0", "A1", )
+STAT_KIND = "E"
 LIMIT = 50
 ORDER = (
     ("R", "R", 0),
+    ("F", "C0", 0),
     ("S", "B1", 0),
     ("F", "B0", 0),
-    ("F", "C0", 0),
+    ("G", "B0", 0),
+    ("F", "A1", 0),
     ("F", "E0", 0),
+    ("S", "A0", 0),
     ("F", "D0", 0),
-    ("S", "A1", 0),
+    ("F", "B0", 1),
+    ("F", "D1", 0),
+    ("G", "A1", 0),
+    ("S", "A2", 0),
+    ("F", "A1", 1),
     ("F", "A0", 0),
-    ("F", "B0", 1),
     ("F", "B1", 0),
-    ("F", "C1", 0),
+    ("G", "B0", 1),
+    ("F", "B0", 2),
+    ("G", "A0", 0),
+    ("F", "A2", 0),
+    ("G", "E0", 0),
+    ("G", "A2", 0),
+    ("F", "E0", 1),
+    ("F", "A0", 1),
+    ("G", "E0", 1),
     ("S", "B2", 0),
-    ("F", "A1", 0),
-    ("F", "A0", 1),
-    ("S", "A2", 0),
+    ("G", "A0", 1),
+    ("S", "B5", 0),
+    ("G", "A1", 1),
+    ("F", "A1", 2),
+    ("G", "B1", 0),
+    ("G", "C0", 0),
+    ("F", "A2", 1),
+    ("S", "E1", 0),
+    ("F", "E0", 2),
+    ("F", "B1", 1),
+    ("F", "B3", 0),
+    ("G", "B1", 1),
+    ("G", "D0", 0),
     ("S", "T", 0),
-    ("F", "D1", 0),
-    ("F", "B1", 1),
+    ("F", "E1", 0),
+    ("S", "B4", 0),
+    ("F", "B1", 2),
+    ("G", "B3", 0),
     ("F", "B2", 0),
-    ("S", "B5", 0),
-    ("F", "B0", 2),
-    ("S", "B4", 0),
-    ("F", "A1", 1),
-    ("F", "B3", 0),
-    ("F", "A2", 0),
-    ("S", "A3", 0),
-    ("F", "C1", 1),
+    ("G", "A1", 2),
+    ("G", "E1", 0),
+    ("F", "B3", 1),
+    ("F", "A0", 2),
     ("F", "T", 0),
-    ("F", "E0", 1),
-    ("F", "A0", 2),
+    ("F", "E1", 1),
+    ("G", "B2", 0),
+    ("F", "D0", 1),
+    ("G", "D1", 0),
+    ("G", "D0", 1),
     ("F", "B5", 0),
     ("F", "B2", 1),
-    ("F", "B1", 2),
+    ("G", "T", 0),
+    ("G", "A2", 1),
+    ("G", "B0", 2),
+    ("G", "B5", 0),
+    ("F", "A2", 2),
+    ("F", "B0", 3),
+    ("G", "E0", 2),
+    ("G", "A2", 2),
+    ("F", "A1", 3),
+    ("F", "B4", 0),
+    ("F", "C0", 1),
+    ("G", "B4", 0),
+    ("G", "E1", 1),
     ("F", "D1", 1),
-    ("F", "C0", 1),
-    ("F", "B3", 1),
-    ("F", "A1", 2),
-    ("F", "A3", 0),
-    ("F", "B0", 3),
+    ("F", "B5", 1),
+    ("G", "B2", 1),
+    ("F", "E1", 2),
+    ("F", "B4", 1),
+    ("G", "B3", 1),
     ("F", "T", 1),
-    ("F", "B4", 0),
-    ("F", "A2", 1),
-    ("F", "D0", 1),
-    ("F", "C1", 2),
-    ("F", "E0", 2),
-    ("F", "B5", 1),
+    ("F", "B2", 2),
+    ("G", "T", 1),
+    ("G", "C0", 1),
+    ("F", "B3", 2),
+    ("G", "D1", 1),
+    ("F", "D0", 2),
+    ("F", "C0", 2),
+    ("G", "B5", 1),
     ("F", "D1", 2),
-    ("F", "B2", 2),
-    ("F", "C0", 2),
-    ("F", "A3", 1),
-    ("F", "B3", 2),
-    ("F", "D0", 2),
-    ("F", "B4", 1),
-    ("F", "A2", 2),
+    ("G", "A0", 2),
+    ("F", "E0", 3),
+    ("G", "B2", 2),
+    ("F", "A2", 3),
+    ("F", "T", 2),
+    ("G", "B4", 1),
+    ("G", "B1", 2),
     ("F", "B5", 2),
-    ("F", "T", 2),
+    ("F", "B4", 2),
+    ("G", "B5", 2),
+    ("G", "T", 2),
+    ("F", "B1", 3),
+    ("F", "T", 3),
+    ("F", "A0", 3),
+    ("G", "E1", 2),
+    ("G", "B4", 2),
+    ("G", "D0", 2),
+    ("F", "E1", 3),
+    ("F", "D0", 3),
+    ("G", "D1", 2),
+    ("G", "B3", 2),
+    ("G", "C0", 2),
+    ("F", "B3", 3),
+    ("F", "B5", 3),
+    ("F", "C0", 3),
     ("F", "B2", 3),
-    ("F", "A3", 2),
-    ("F", "B1", 3),
-    ("F", "C0", 3),
-    ("F", "A0", 3),
-    ("F", "B4", 2),
     ("F", "D1", 3),
-    ("F", "T", 3),
-    ("F", "E0", 3),
-    ("F", "A2", 3),
-    ("F", "A3", 3),
-    ("F", "C1", 3),
-    ("F", "D0", 3),
-    ("F", "B5", 3),
-    ("F", "A1", 3),
-    ("F", "B3", 3),
     ("F", "B4", 3),
 )
 
@@ -196,6 +237,10 @@
     return sizes["z"] >> done
 
 
+def parts_of(order, phase):
+    return 2 if phase + 1 < len(order) else 1
+
+
 def tiles_sent(sizes, order, phase):
     kept, sent = exchange(sizes, order, phase)
     return len(kept) * len(sent) * slots_of(sizes, order, phase)
@@ -218,7 +263,8 @@
     for p in pieces(sizes).values():
         for phase in range(len(p.order)):
             send.setdefault((p.stat, tiles_sent(sizes, p.order, phase)), len(send))
-            recv[p.name, phase] = len(recv)
+            for part in range(parts_of(p.order, phase)):
+                recv[p.name, phase, part] = len(recv)
     return recv, send
 
 
@@ -230,6 +276,7 @@
     )
     span = Z * tile
     halves = span // step
+    assert halves <= 2
     per = step // tile
     rows = lax.axis_index("rows")
     z = lax.axis_index("grp")
@@ -397,7 +444,17 @@
     def array(p):
         return (stat, LANES) if p.stat else (acc, tile)
 
-    def columns(p, phase, away):
+    def split(p, phase, part):
+        kept = exchange(cfg, p.order, phase)[0]
+        if phase + 1 == len(p.order):
+            return list(range(len(kept))), None
+        follow = p.order[phase + 1]
+        if follow not in "xy":
+            return list(range(len(kept))), follow
+        i = "xy".index(follow)
+        return [k for k, g in enumerate(kept) if (g[i] == 0) == (part == 1)], None
+
+    def columns(p, phase, part, away):
         unit = array(p)[1]
         low = 0
         for axis in p.order[:phase]:
@@ -407,44 +464,55 @@
         count = slots_of(cfg, p.order, phase)
         if axis not in "xy":
             low += (1 - bit(axis) if away else bit(axis)) * count
-        if isinstance(low, int):
-            return pl.ds(low * unit, count * unit)
-        return pl.ds(pl.multiple_of(low * unit, unit), count * unit)
-
-    def copy(p, phase, d, k, g, cols, part=None):
-        src = array(p)[0]
-        dst = ref_of[p.name, phase].at[d, k]
-        if part is not None:
-            dst = ref_of[p.name, phase].at[d, k, :, part]
+        inner, follow = 0, split(p, phase, part)[1]
+        if follow:
+            count //= 2
+            inner = (bit(follow) if part else 1 - bit(follow)) * count
+
+        def cut(at):
+            if isinstance(at, int):
+                return pl.ds(at * unit, count * unit)
+            return pl.ds(pl.multiple_of(at * unit, unit), count * unit)
+
+        return cut(low + inner), cut(inner)
+
+    def copy(p, phase, part, d, k, g, cols, there):
         return pltpu.make_async_remote_copy(
-            src_ref=src.at[quad(g), pl.ds(p.start, p.height), cols],
-            dst_ref=dst,
+            src_ref=array(p)[0].at[quad(g), pl.ds(p.start, p.height), cols],
+            dst_ref=ref_of[p.name, phase].at[d, k, :, there],
             send_sem=send_sem.at[outgoing[p.stat, tiles_sent(cfg, p.order, phase)]],
-            recv_sem=recv_sem.at[incoming[p.name, phase]],
+            recv_sem=recv_sem.at[incoming[p.name, phase, part]],
             device_id=peer(p.order[phase], d + 1),
             device_id_type=MESH,
         )
 
-    def begin(p, phase):
-        if phase < len(p.order):
-            cols = columns(p, phase, True)
+    def begin(p, phase, only=None):
+        if phase == len(p.order):
+            return
+        for part in range(parts_of(p.order, phase)):
+            cols, there = columns(p, phase, part, True)
             for d, quads in enumerate(exchange(cfg, p.order, phase)[1]):
-                for k, g in enumerate(quads):
-                    copy(p, phase, d, k, g, cols).start()
-
-    def finish(p, phase):
+                for k in split(p, phase, part)[0]:
+                    if only is None or quads[k] == only:
+                        copy(p, phase, part, d, k, quads[k], cols, there).start()
+
+    def finish(p, phase, part):
         src = array(p)[0]
         kept, sent = exchange(cfg, p.order, phase)
-        if not sent:
+        touched = split(p, phase, part)[0]
+        if not sent or not touched:
             return
         ref = ref_of[p.name, phase]
-        arrived(ref, recv_sem.at[incoming[p.name, phase]])
-        cols = columns(p, phase, False)
-        for k, g in enumerate(kept):
-            where = (quad(g), pl.ds(p.start, p.height), cols)
+        cols, there = columns(p, phase, part, False)
+        arrived(
+            ref.at[:, pl.ds(0, len(touched)), :, pl.ds(0, cols.size)],
+            recv_sem.at[incoming[p.name, phase, part]],
+        )
+        for k in touched:
+            where = (quad(kept[k]), pl.ds(p.start, p.height), cols)
             total = src[where]
             for d in range(len(sent)):
-                total = total + ref[d, k]
+                total = total + ref[d, k, :, there]
             src[where] = total
 
     links = []
@@ -489,24 +557,19 @@
 
     def first_sends(p, g, h):
         axis = p.order[0]
-        for d, quads in enumerate(exchange(cfg, p.order, 0)[1]):
-            if g not in quads:
+        if halves == 1 or axis not in "xy":
+            if h == 0:
+                begin(p, 0, g)
+            return
+        for part in range(2):
+            touched, follow = split(p, 0, part)
+            if follow and part != h:
                 continue
-            k = quads.index(g)
-            if axis in "xy":
-                part = span_of(h, step)
-                copy(p, 0, d, k, g, part, part if halves > 1 else None).start()
-            elif halves == 1:
-                copy(p, 0, d, k, g, columns(p, 0, True)).start()
-            elif halves == 2:
-                if h == 0:
-                    copy(p, 0, d, k, g, span_of(h, step)).start()
-            else:
-
-                @pl.when(bit(axis) == 1 - 2 * h // halves)
-                def _():
-                    part = pl.ds(h * step % (span // 2), step)
-                    copy(p, 0, d, k, g, pl.ds(h * step, step), part).start()
+            for d, quads in enumerate(exchange(cfg, p.order, 0)[1]):
+                for k in touched:
+                    if quads[k] == g:
+                        cols = span_of(h, step)
+                        copy(p, 0, part, d, k, g, cols, cols).start()
 
     def add_rows(n, rows):
         g, h = units[n]
@@ -576,14 +639,20 @@
         p = made[op[1]]
         if op[0] == "S":
             begin(p, 0)
-        elif op[2] < len(p.order):
+        elif op[0] == "F":
             with scope(f"F{op[1]}.{op[2]}"):
-                finish(p, op[2])
+                finish(p, op[2], 0)
                 begin(p, op[2] + 1)
+        else:
+            with scope(f"G{op[1]}.{op[2]}"):
+                finish(p, op[2], 1)
     for p in made.values():
-        for phase in range(4, len(p.order)):
-            finish(p, phase)
-            begin(p, phase + 1)
+        for phase in range(PHASES - 1, len(p.order)):
+            if phase >= PHASES:
+                finish(p, phase, 0)
+                begin(p, phase + 1)
+            if parts_of(p.order, phase) == 2:
+                finish(p, phase, 1)
 
     with scope("final"):
         own = y * X + x

time: 72.8 us -> 71.8 us (0.986)
  Pallas kernels: 71.8 us -> 70.8 us
    pallas_call x1, Pallas kernels: 71.8 us -> 70.8 us  [shards(): pl.pallas_call(functools.partial(kernel, cfg), out_shape=jax.ShapeDtypeSt...]
where the time goes in v3:
time: 71.8 us; the launch traced here: 71.6 us
  Pallas kernels  70.8 us (99%)
  local copies, waits for them, and re-layouts  0.8 us (1%)
    pallas_call x1, Pallas kernels, shards(): pl.pallas_call(functools.partial(kernel, cfg), out_shape=jax.ShapeDtypeSt...  70.8 us

profile of v3, /device:TPU:0, one launch (start us, length us, event | category | flops | bytes accessed | tf_op | source)
XLA Modules:
  0.0 71.6 jit_solution(6804345589240855855)
XLA Ops:
  0.0 70.8 %shard_map.28 = f32[512,256]{1,0:T(8,128)S(1)} custom-call(bf16[768,16384]{1,0:T(8,128)(2,1)} %matrix_ref.1, s32[16,768]{1,0:T(8,128)} %keep_hbm.1), custom_call_target="tpu_custom_call" | custom-call | flops 6442450944 | bytes 25165824 | tf_op jit(solution)/shard_map/pallas_call | solution.py:704
  70.8 0.8 %copy.4 = f32[512,256]{1,0:T(8,128)} copy(f32[512,256]{1,0:T(8,128)S(1)} %shard_map.28) | data formatting | bytes 1048576
